TPU v7x, 128 devices: a whole 4x4x4 slice. The times are simulated.
128 devices in a mesh: tm: 16 (over z, y_lo, core), member: 8 (over x, y_hi).
Axes of the slice: x: 4, y: 4 (y_hi: 2, y_lo: 2; y = y_hi * 2 + y_lo), z: 4, core: 2. Of those that a mesh axis runs over, the one named last changes fastest.
Arguments:
- fields: float32 [48, 96, 16384], P('member', 'tm'), may hold values from 200 to 350, as said below
Outputs:
- covariance: float32 [48, 48, 16384], P('member', None, 'tm')
Inputs may be any that keep to these rules, and one draw needn't show every extreme that they name: `fields`: month t is calendar month t mod 12.
All inputs are finite; a program needn't handle non-finite values.
Results may differ from a plain program's by a relative error of at most 0.0003.
Values sent between devices are 32-bit elements; how exact they have to be, the bound alone decides.
A program may use at most 192 MiB of HBM per device.

v0:
```python
import jax
import jax.numpy as jnp
from jax import lax
from jax.sharding import PartitionSpec as P


def cut_along(shard, dim, size):
    before, after = (shard.shape[:dim], shard.shape[dim + 1 :])
    return jnp.moveaxis(shard.reshape(*before, size, -1, *after), dim, 0)


def joined_along(pieces, dim):
    lengths = list(pieces.shape[1:])
    lengths[dim] *= pieces.shape[0]
    return jnp.moveaxis(pieces, 0, dim).reshape(lengths)


def joined_exchange(shard, axis, axes, splits, concats):
    sizes = [lax.axis_size(a) for a in axes]
    pieces = cut_along(shard, splits[0], sizes[0])
    pieces = jnp.moveaxis(cut_along(pieces, splits[1] + 1, sizes[1]), 0, 1)
    inside = pieces.shape[2:]
    pieces = pieces.reshape(-1, *inside)
    pieces = lax.all_to_all(pieces, axis, split_axis=0, concat_axis=0, tiled=True)
    pieces = joined_along(pieces.reshape(*sizes, *inside), concats[0] + 1)
    return joined_along(pieces, concats[1])


def monthly_anomaly(series):
    members_here, months_here, pixel_count = series.shape
    by_year = series.reshape(members_here, months_here // 12, 12, pixel_count)
    climatology = jnp.mean(by_year, axis=1, keepdims=True)
    return (by_year - climatology).reshape(members_here, months_here, pixel_count)


def cross_block(first_rows, second_rows, divisor):
    products = jnp.einsum(
        "itp,jtp->ijp",
        first_rows,
        second_rows,
        precision=lax.Precision.HIGHEST,
        preferred_element_type=jnp.float32,
    )
    return products / divisor


def per_device(fields):
    members_here, mon_here, pixel_count = fields.shape
    tm_count = lax.axis_size("tm")
    divisor = float(mon_here * tm_count - 12)
    regrouped = joined_exchange(fields, ("tm", "member"), ("tm", "member"), (2, 2), (1, 0))
    anomaly = monthly_anomaly(regrouped)
    whole_block = cross_block(anomaly, anomaly, divisor)
    return lax.all_to_all(whole_block, "member", split_axis=0, concat_axis=2, tiled=True)


def solution(mesh):
    in_specs = (P("member", "tm", None),)
    out_specs = P("member", None, "tm")
    return jax.shard_map(
        per_device, mesh=mesh, in_specs=in_specs, out_specs=out_specs, check_vma=False
    )
```

profile of v0, /device:TPU:1, one launch (start us, length us, event | category | flops | bytes accessed | tf_op | source)
XLA Modules:
  0.0 106.1 jit_solution(14046053238351109429)
XLA Ops:
  0.0 2.7 %reshape.19 = f32[6,6,16,1024]{3,2,1,0:T(8,128)S(1)} reshape(f32[6,6,16384]{2,1,0:T(8,128)} %param.1) | data formatting | bytes 4718592 | tf_op jit(solution)/shard_map/reshape | solution.py:9
  2.7 0.5 copy.36
  3.2 1.4 %copy.24 = f32[128,6,6,128]{3,2,1,0:T(8,128)S(1)} copy(f32[128,6,6,128]{3,0,2,1:T(8,128)S(1)} %bitcast.34) | data formatting | bytes 4718592 | tf_op jit(solution)/shard_map/reshape | solution.py:23
  4.6 53.0 %all_to_all.23 = f32[128,6,6,128]{3,2,1,0:T(8,128)S(1)} all-to-all(f32[128,6,6,128]{3,2,1,0:T(8,128)S(1)} %copy.24), channel_id=1, replica_groups=mesh['tm'=16,'member'=8] {'tm','member'}, dimensions={0} | all-to-all | bytes 4718592 | tf_op jit(solution)/shard_map/all_to_all | solution.py:24
  57.6 2.2 %copy.27 = f32[8,6,16,6,128]{4,1,0,3,2:T(8,128)} copy(f32[8,6,16,6,128]{4,3,1,0,2:T(8,128)S(1)} %bitcast.31) | data formatting | bytes 4718592 | tf_op jit(solution)/shard_map/transpose | solution.py:15
  59.8 0.4 copy.26
  60.2 4.0 %reshape_reshape_reshape.6 = f32[48,8,12,128]{3,0,2,1:T(8,128)} reshape(f32[8,6,16,6,128]{4,1,0,3,2:T(8,128)} %copy.27) | data formatting | bytes 4718592 | tf_op jit(solution)/shard_map/reshape;reshape;reshape | solution.py:31
  64.2 2.5 %reduce_sum.9 = f32[48,12,128]{2,0,1:T(8,128)} reduce(f32[48,8,12,128]{3,0,2,1:T(8,128)} %reshape_reshape_reshape.6, f32[]{:T(128)} %constant.2.clone.1), dimensions={1}, to_apply=%region_0.0 | reduce | flops 516096 | bytes 2654212 | tf_op jit(solution)/shard_map/reduce_sum | solution.py:32
  66.8 1.0 broadcast_multiply_fusion
  67.8 1.6 %reshape_reshape_reshape.5 = f32[48,96,128]{2,1,0:T(8,128)} reshape(f32[8,6,16,6,128]{4,3,2,1,0:T(8,128)S(1)} %copy.26) | data formatting | bytes 4718592 | tf_op jit(solution)/shard_map/reshape;reshape;reshape | solution.py:31
  69.3 0.0 copy-start
  69.3 0.2 sub.11
  69.5 1.5 %copy-done = f32[48,96,128]{2,1,0:T(8,128)S(1)} copy-done((f32[48,96,128]{2,1,0:T(8,128)S(1)}, f32[48,96,128]{2,1,0:T(8,128)}, u32[]{:S(2)}) %copy-start) | copy-done | bytes 2359320
  71.0 2.2 %copy_subtract_fusion = f32[48,96,128]{2,1,0:T(8,128)} fusion(f32[48,96,128]{2,1,0:T(8,128)S(1)} %copy-done, f32[48,96,128]{2,0,1:T(8,128)S(1)} %bitcast.33), kind=kLoop, calls=%fused_computation.1 | loop fusion | flops 589824 | bytes 7077888 | tf_op jit(solution)/shard_map/sub | solution.py:33
  73.2 2.4 %copy.29 = f32[48,96,128]{1,0,2:T(8,128)S(1)} copy(f32[48,96,128]{2,1,0:T(8,128)} %copy_subtract_fusion) | data formatting | bytes 4718592 | tf_op jit(solution)/shard_map/sub | solution.py:33
  75.6 6.8 %multiply_bitcast_fusion = f32[48,48,128]{0,1,2:T(8,128)} fusion(f32[48,96,128]{1,0,2:T(8,128)S(1)} %copy.29), kind=kOutput, calls=%fused_computation | convolution fusion | flops 340033536 | bytes 3538944 | tf_op jit(solution)/shard_map/itp,jtp->ijp/dot_general | solution.py:37
  82.5 2.4 %copy.31 = f32[48,48,128]{2,1,0:T(8,128)S(1)} copy(f32[48,48,128]{0,1,2:T(8,128)} %multiply_bitcast_fusion) | data formatting | bytes 2359296 | tf_op jit(solution)/shard_map/div | solution.py:44
  84.9 20.1 %all_to_all.24 = f32[48,48,128]{2,1,0:T(8,128)S(1)} all-to-all(f32[48,48,128]{2,1,0:T(8,128)S(1)} %copy.31), channel_id=1, replica_groups=mesh['tm'=16,'member'=8] {'member'}, dimensions={0} | all-to-all | bytes 2359296 | tf_op jit(solution)/shard_map/all_to_all | solution.py:54
  104.9 1.2 %copy.39 = f32[8,6,6,8,128]{4,3,0,2,1:T(8,128)} copy(f32[8,6,6,8,128]{4,3,2,1,0:T(8,128)S(1)} %bitcast.36) | data formatting | bytes 2359296 | tf_op jit(solution)/shard_map/all_to_all | solution.py:54
Async XLA Ops:
  69.3 1.7 %copy-start = (f32[48,96,128]{2,1,0:T(8,128)S(1)}, f32[48,96,128]{2,1,0:T(8,128)}, u32[]{:S(2)}) copy-start(f32[48,96,128]{2,1,0:T(8,128)} %reshape_reshape_reshape.5) | copy-start | bytes 7077892
where the time goes:
time: 107 us; the launch traced here: 106 us
  blocking collectives  73 us (68%)
  local copies, waits for them, and re-layouts  20.5 us (19%)
  matrix products  6.82 us (6%)
  other arithmetic  5.72 us (5%)
    all_to_all x1, blocking collectives, joined_exchange(): lax.all_to_all(pieces, axis, split_axis=0, concat_axis=0, tiled=True)  53 us
    all_to_all x1, blocking collectives, per_device(): lax.all_to_all(whole_block, 'member', split_axis=0, concat_axis=2, tiled=...  20.1 us
    dot_general x1, matrix products, cross_block(): jnp.einsum('itp,jtp->ijp', first_rows, second_rows, precision=lax.Precisi...  6.82 us
    another operation x2, local copies, waits for them, and re-layouts, monthly_anomaly(): by_year = series.reshape(members_here, months_here // 12, 12, pixel_count)  5.57 us
    reshape x1, local copies, waits for them, and re-layouts, cut_along(): return jnp.moveaxis(shard.reshape(*before, size, -1, *after), dim, 0)  2.65 us
    sub x2, local copies, waits for them, and re-layouts, monthly_anomaly(): by_year - climatology  2.62 us
    transpose x2, local copies, waits for them, and re-layouts, joined_along(): return jnp.moveaxis(pieces, 0, dim).reshape(lengths)  2.61 us
    reduce_sum x1, other arithmetic, monthly_anomaly(): climatology = jnp.mean(by_year, axis=1, keepdims=True)  2.53 us

commit v1 on v0

v1 whole, which is shorter than its diff:
```python
import functools

import jax
import jax.numpy as jnp
from jax import lax
from jax.experimental import pallas as pl
from jax.experimental.pallas import tpu as pltpu
from jax.sharding import PartitionSpec as P

MESH = pl.DeviceIdType.MESH
F32 = jnp.float32
ORDER = ((2, 1), (2, 0), (1, 1), (3, 1), (1, 0), (3, 0), (0, 1), (0, 0))
LAST = len(ORDER) - 1


def contrasts(years):
    shifted = [y - years[0] for y in years[1:]]
    a1, a2, a3, a4, a5, a6, a7 = shifted
    p0, m0 = a4, -a4
    p1, m1 = a1 + a5, a1 - a5
    p2, m2 = a2 + a6, a2 - a6
    p3, m3 = a3 + a7, a3 - a7
    out = []
    q0, q2, q1, q3 = p0 + p2, p0 - p2, p1 + p3, p1 - p3
    out += [q0 - q1, q2 + q3, q2 - q3]
    r0, r2, r1, r3 = m0 + m2, m0 - m2, m1 + m3, m1 - m3
    out += [r0 + r1, r0 - r1, r2 + r3, r2 - r3]
    return out


def kernel(sizes, fields, out, raw, con, blk, got, send1, recv1, own, send3, recv3):
    tms, members, rows, mons, scale = sizes
    t, m = lax.axis_index("tm"), lax.axis_index("member")
    me = t * members + m
    total = tms * members
    x, h = m // 2, m % 2
    ten, low, core = t // 4, (t // 2) % 2, t % 2

    barrier = pltpu.get_barrier_semaphore()

    @pl.loop(1, total)
    def _(p):
        d = (me + p) % total
        pl.semaphore_signal(barrier, inc=1, device_id=(d // members, d % members), device_id_type=MESH)

    def pixels(d):
        return pl.ds(pl.multiple_of(d * 128, 128), 128)

    mine = pltpu.make_async_copy(fields.at[:, :, pixels(me)], raw.at[LAST * tms + t], own)
    mine.start()

    @pl.loop(0, con.shape[0])
    def _(s):
        con[s] = jnp.zeros(con.shape[1:], F32)

    pl.semaphore_wait(barrier, total - 1)

    for s, (dx, dh) in enumerate(ORDER):
        to_m = ((x + 4 - dx) % 4) * 2 + (h + dh) % 2

        @pl.loop(1 if s == LAST else 0, tms)
        def _(q, s=s, to_m=to_m):
            to_t = ((ten + q // 4) % 4) * 4 + ((low + (q // 2) % 2) % 2) * 2 + (core + q % 2) % 2
            pltpu.make_async_remote_copy(
                src_ref=fields.at[:, :, pixels(to_t * members + to_m)],
                dst_ref=raw.at[s * tms + t],
                send_sem=send1,
                recv_sem=recv1.at[s],
                device_id=(to_t, to_m),
                device_id_type=MESH,
            ).start()

    group = [((x + dx) % 4) * 2 + (h + dh) % 2 for dx, dh in ORDER]

    def transform(s):
        @pl.loop(0, rows)
        def _(i):
            for half in range(2):
                years = [raw[s * tms + 2 * y + half, i] for y in range(tms // 2)]
                for q, c in enumerate(contrasts(years)):
                    con[s, half * 7 + q, i, 0:mons] = c

    lane_row = lax.broadcasted_iota(jnp.int32, (8, 128), 0)

    def block(s, s2):
        cols = [jnp.zeros((8, 128), F32) for _ in range(rows)]
        for base in range(0, rows, 3):
            acc = [[None] * rows for _ in range(3)]
            for q in range(14):
                left = [con[s, q, base + a] for a in range(3)]
                right = [con[s2, q, b] for b in range(rows)]
                for a in range(3):
                    for b in range(rows):
                        prod = left[a] * right[b]
                        acc[a][b] = prod if q == 0 else acc[a][b] + prod
            for a in range(3):
                line = jnp.zeros((8, 128), F32)
                for b in range(rows):
                    r = jnp.sum(acc[a][b], axis=0, keepdims=True) * scale
                    r = jnp.broadcast_to(r, (8, 128))
                    line = jnp.where(lane_row == b, r, line)
                    cols[b] = jnp.where(lane_row == base + a, r, cols[b])
                blk[s, s2, base + a] = line[0:rows]
        for b in range(rows):
            blk[s2, s, b] = cols[b][0:rows]

    def ship(a, b):
        if a == LAST:
            return
        pltpu.make_async_remote_copy(
            src_ref=blk.at[a, b],
            dst_ref=got.at[m, group[b]],
            send_sem=send3,
            recv_sem=recv3,
            device_id=(t, group[a]),
            device_id_type=MESH,
        ).start()

    pending = []
    for s in range(len(ORDER)):
        if s == LAST:
            mine.wait()
        n = tms - 1 if s == LAST else tms
        landed = raw.at[pl.ds(s * tms, n)]
        pltpu.make_async_remote_copy(
            src_ref=landed, dst_ref=landed, send_sem=send1, recv_sem=recv1.at[s],
            device_id=(t, m), device_id_type=MESH,
        ).wait_recv()
        transform(s)
        step = 4
        for lo in range(0, s + 1, step):
            hi = min(lo + step, s + 1)

            @pl.loop(lo, hi)
            def _(s2, s=s):
                block(s, s2)

            for a, b in pending:
                ship(a, b)
            pending = []
            for s2 in range(lo, hi):
                pending.append((s, s2))
                if s2 != s:
                    pending.append((s2, s))
    for a, b in pending:
        ship(a, b)
    for b in range(len(ORDER)):
        got[m, group[b]] = blk[LAST, b]

    arrived = got.at[pl.ds(0, members - 1)]
    done = pltpu.make_async_remote_copy(
        src_ref=arrived, dst_ref=arrived, send_sem=send3, recv_sem=recv3,
        device_id=(t, m), device_id_type=MESH,
    )
    done.wait_recv()

    @pl.loop(0, rows)
    def _(i):
        for o in range(members):
            for n in range(members):
                out[i, n * rows:(n + 1) * rows, o * 128:(o + 1) * 128] = got[o, n, i]

    done.wait_send()
    sent = raw.at[pl.ds(0, total - 1)]
    pltpu.make_async_remote_copy(
        src_ref=sent, dst_ref=sent, send_sem=send1, recv_sem=recv1.at[0],
        device_id=(t, m), device_id_type=MESH,
    ).wait_send()


def per_device(fields):
    rows, mons, pixels = fields.shape
    tms, members = lax.axis_size("tm"), lax.axis_size("member")
    scale = 1.0 / (8.0 * float(mons * tms - 12))
    return pl.pallas_call(
        functools.partial(kernel, (tms, members, rows, mons, scale)),
        out_shape=jax.ShapeDtypeStruct((rows, rows * members, pixels // tms), F32),
        in_specs=[pl.BlockSpec(memory_space=pltpu.HBM)],
        out_specs=pl.BlockSpec(memory_space=pltpu.VMEM),
        scratch_shapes=[
            pltpu.VMEM((tms * members, rows, mons, 128), F32),
            pltpu.VMEM((members, 14, rows, 8, 128), F32),
            pltpu.VMEM((members, members, rows, rows, 128), F32),
            pltpu.VMEM((members, members, rows, rows, 128), F32),
            pltpu.SemaphoreType.DMA,
            pltpu.SemaphoreType.DMA((members,)),
            pltpu.SemaphoreType.DMA,
            pltpu.SemaphoreType.DMA,
            pltpu.SemaphoreType.DMA,
        ],
        compiler_params=pltpu.CompilerParams(collective_id=0, has_side_effects=True, vmem_limit_bytes=40 * 2**20),
        name="cov",
    )(fields)


def solution(mesh):
    in_specs = (P("member", "tm", None),)
    out_specs = P("member", None, "tm")
    return jax.shard_map(per_device, mesh=mesh, in_specs=in_specs, out_specs=out_specs, check_vma=False)
```

time: 107 us -> 63.6 us (0.59)
  blocking collectives: 73 us -> 0 us
  Pallas kernels: 0 us -> 60.6 us
  local copies, waits for them, and re-layouts: 20.5 us -> 2.9 us
  matrix products: 6.82 us -> 0 us
  other arithmetic: 5.72 us -> 0 us
    all_to_all x2 -> x0, blocking collectives: 73 us -> none  [the longest x1 53 us: joined_exchange(): lax.all_to_all(pieces, axis, split_axis=0, concat_axis=0, tiled=True)]
    pallas_call x0 -> x1, Pallas kernels: none -> 60.6 us  [per_device(): pl.pallas_call(functools.partial(kernel, (tms, members, rows, mons, scale...]
    dot_general x1 -> x0, matrix products: 6.82 us -> none  [cross_block(): jnp.einsum('itp,jtp->ijp', first_rows, second_rows, precision=lax.Precisi...]
    another operation x2 -> x0, local copies, waits for them, and re-layouts: 5.57 us -> none  [monthly_anomaly(): by_year = series.reshape(members_here, months_here // 12, 12, pixel_count)]
    reshape x2 -> x0, local copies, waits for them, and re-layouts: 4.07 us -> none  [the longest x1 2.65 us: cut_along(): return jnp.moveaxis(shard.reshape(*before, size, -1, *after), dim, 0)]
    sub x2 -> x0, local copies, waits for them, and re-layouts: 2.62 us -> none  [monthly_anomaly(): by_year - climatology]
    transpose x2 -> x0, local copies, waits for them, and re-layouts: 2.61 us -> none  [joined_along(): return jnp.moveaxis(pieces, 0, dim).reshape(lengths)]
    reduce_sum x1 -> x0, other arithmetic: 2.53 us -> none  [monthly_anomaly(): climatology = jnp.mean(by_year, axis=1, keepdims=True)]
where the time goes in v1:
time: 63.6 us; the launch traced here: 63.5 us
  Pallas kernels  60.6 us (95%)
  local copies, waits for them, and re-layouts  2.9 us (5%)
    pallas_call x1, Pallas kernels, per_device(): pl.pallas_call(functools.partial(kernel, (tms, members, rows, mons, scale...  60.6 us
    unnamed x3, local copies, waits for them, and re-layouts  2.9 us

profile of v1, /device:TPU:1, one launch (start us, length us, event | category | flops | bytes accessed | tf_op | source)
XLA Modules:
  0.0 63.5 jit_solution(11550816559697525385)
XLA Ops:
  0.0 0.0 copy-start
  0.0 1.9 %copy-done = f32[6,6,16384]{2,1,0:T(8,128)S(1)} copy-done((f32[6,6,16384]{2,1,0:T(8,128)S(1)}, f32[6,6,16384]{2,1,0:T(8,128)}, u32[]{:S(2)}) %copy-start) | copy-done | bytes 2359320
  1.9 60.6 %cov.1 = f32[6,48,1024]{2,1,0:T(8,128)S(1)} custom-call(f32[6,6,16384]{2,1,0:T(8,128)S(1)} %copy-done), custom_call_target="tpu_custom_call" | custom-call | tf_op jit(solution)/shard_map/cov/pallas_call | solution.py:175
  62.5 1.0 %copy.3 = f32[6,48,1024]{2,1,0:T(8,128)} copy(f32[6,48,1024]{2,1,0:T(8,128)S(1)} %cov.1) | data formatting | bytes 2359296
Async XLA Ops:
  0.0 1.9 %copy-start = (f32[6,6,16384]{2,1,0:T(8,128)S(1)}, f32[6,6,16384]{2,1,0:T(8,128)}, u32[]{:S(2)}) copy-start(f32[6,6,16384]{2,1,0:T(8,128)} %fields.1) | copy-start | bytes 7077892

commit v2 on v1

--- a/solution.py
+++ b/solution.py
@@ -9,8 +9,21 @@
 
 MESH = pl.DeviceIdType.MESH
 F32 = jnp.float32
-ORDER = ((2, 1), (2, 0), (1, 1), (3, 1), (1, 0), (3, 0), (0, 1), (0, 0))
-LAST = len(ORDER) - 1
+ORDER = ((1, 1), (3, 0), (1, 0), (3, 1), (0, 0), (2, 1), (0, 1), (2, 0))
+SELF = ORDER.index((0, 0))
+SENDS = (
+    (1, 1), (0, 9), (1, 0), (0, 8), (0, 3), (1, 10), (1, 13), (0, 5), (1, 4), (0, 12), (1, 3), (0, 10),
+    (1, 5), (0, 13), (1, 11), (0, 2), (0, 4), (1, 12), (1, 2), (0, 11), (0, 7), (1, 14), (0, 0), (1, 9),
+    (0, 14), (1, 7), (1, 6), (0, 15), (0, 6), (1, 15), (0, 1), (1, 8), (2, 0), (3, 9), (2, 1), (3, 8),
+    (2, 3), (3, 10), (3, 13), (2, 5), (3, 4), (2, 12), (3, 3), (2, 10), (3, 5), (2, 13), (3, 11), (2, 2),
+    (2, 4), (3, 12), (3, 2), (2, 11), (2, 7), (3, 14), (2, 14), (3, 7), (3, 1), (2, 9), (3, 6), (2, 15),
+    (2, 6), (3, 15), (3, 0), (2, 8), (5, 9), (4, 1), (5, 8), (4, 4), (5, 13), (4, 2), (5, 10), (4, 5),
+    (5, 12), (4, 13), (5, 5), (4, 3), (5, 11), (4, 12), (5, 4), (4, 15), (5, 7), (4, 6), (5, 14), (4, 7),
+    (5, 15), (4, 8), (5, 0), (4, 14), (5, 6), (4, 9), (5, 1), (5, 3), (4, 10), (4, 11), (5, 2), (6, 3),
+    (7, 10), (6, 2), (7, 11), (7, 7), (6, 14), (7, 0), (6, 9), (7, 14), (6, 7), (6, 1), (7, 9), (6, 6),
+    (7, 15), (7, 6), (6, 15), (6, 0), (7, 8), (7, 1), (6, 8), (7, 3), (6, 10), (6, 13), (7, 5), (6, 4),
+    (7, 12), (6, 5), (7, 13), (6, 11), (7, 2), (7, 4), (6, 12),
+)
 
 
 def contrasts(years):
@@ -38,15 +51,17 @@
 
     barrier = pltpu.get_barrier_semaphore()
 
-    @pl.loop(1, total)
-    def _(p):
-        d = (me + p) % total
-        pl.semaphore_signal(barrier, inc=1, device_id=(d // members, d % members), device_id_type=MESH)
+    near_t = [((ten + q // 4) % 4) * 4 + ((low + (q // 2) % 2) % 2) * 2 + (core + q % 2) % 2 for q in range(tms)]
+    from_m = [((x + dx) % 4) * 2 + (h + dh) % 2 for dx, dh in ORDER]
+    to_m = [((x + 4 - dx) % 4) * 2 + (h + dh) % 2 for dx, dh in ORDER]
+
+    for s, q in SENDS:
+        pl.semaphore_signal(barrier, inc=1, device_id=(near_t[q], to_m[s]), device_id_type=MESH)
 
     def pixels(d):
         return pl.ds(pl.multiple_of(d * 128, 128), 128)
 
-    mine = pltpu.make_async_copy(fields.at[:, :, pixels(me)], raw.at[LAST * tms + t], own)
+    mine = pltpu.make_async_copy(fields.at[:, :, pixels(me)], raw.at[SELF * tms + t], own)
     mine.start()
 
     @pl.loop(0, con.shape[0])
@@ -55,22 +70,15 @@
 
     pl.semaphore_wait(barrier, total - 1)
 
-    for s, (dx, dh) in enumerate(ORDER):
-        to_m = ((x + 4 - dx) % 4) * 2 + (h + dh) % 2
-
-        @pl.loop(1 if s == LAST else 0, tms)
-        def _(q, s=s, to_m=to_m):
-            to_t = ((ten + q // 4) % 4) * 4 + ((low + (q // 2) % 2) % 2) * 2 + (core + q % 2) % 2
-            pltpu.make_async_remote_copy(
-                src_ref=fields.at[:, :, pixels(to_t * members + to_m)],
-                dst_ref=raw.at[s * tms + t],
-                send_sem=send1,
-                recv_sem=recv1.at[s],
-                device_id=(to_t, to_m),
-                device_id_type=MESH,
-            ).start()
-
-    group = [((x + dx) % 4) * 2 + (h + dh) % 2 for dx, dh in ORDER]
+    for s, q in SENDS:
+        pltpu.make_async_remote_copy(
+            src_ref=fields.at[:, :, pixels(near_t[q] * members + to_m[s])],
+            dst_ref=raw.at[s * tms + t],
+            send_sem=send1,
+            recv_sem=recv1.at[s],
+            device_id=(near_t[q], to_m[s]),
+            device_id_type=MESH,
+        ).start()
 
     def transform(s):
         @pl.loop(0, rows)
@@ -105,22 +113,22 @@
             blk[s2, s, b] = cols[b][0:rows]
 
     def ship(a, b):
-        if a == LAST:
+        if a == SELF:
             return
         pltpu.make_async_remote_copy(
             src_ref=blk.at[a, b],
-            dst_ref=got.at[m, group[b]],
+            dst_ref=got.at[m, from_m[b]],
             send_sem=send3,
             recv_sem=recv3,
-            device_id=(t, group[a]),
+            device_id=(t, from_m[a]),
             device_id_type=MESH,
         ).start()
 
     pending = []
     for s in range(len(ORDER)):
-        if s == LAST:
+        if s == SELF:
             mine.wait()
-        n = tms - 1 if s == LAST else tms
+        n = tms - 1 if s == SELF else tms
         landed = raw.at[pl.ds(s * tms, n)]
         pltpu.make_async_remote_copy(
             src_ref=landed, dst_ref=landed, send_sem=send1, recv_sem=recv1.at[s],
@@ -145,7 +153,7 @@
     for a, b in pending:
         ship(a, b)
     for b in range(len(ORDER)):
-        got[m, group[b]] = blk[LAST, b]
+        got[m, from_m[b]] = blk[SELF, b]
 
     arrived = got.at[pl.ds(0, members - 1)]
     done = pltpu.make_async_remote_copy(

time: 63.6 us -> 55.7 us (0.88)
  Pallas kernels: 60.6 us -> 52.7 us
    pallas_call x1, Pallas kernels: 60.6 us -> 52.7 us  [per_device(): pl.pallas_call(functools.partial(kernel, (tms, members, rows, mons, scale...]
where the time goes in v2:
time: 55.7 us; the launch traced here: 55.6 us
  Pallas kernels  52.7 us (95%)
  local copies, waits for them, and re-layouts  2.9 us (5%)
    pallas_call x1, Pallas kernels, per_device(): pl.pallas_call(functools.partial(kernel, (tms, members, rows, mons, scale...  52.7 us
    unnamed x3, local copies, waits for them, and re-layouts  2.9 us

profile of v2, /device:TPU:1, one launch (start us, length us, event | category | flops | bytes accessed | tf_op | source)
XLA Modules:
  0.0 55.6 jit_solution(15293580814476988669)
XLA Ops:
  0.0 0.0 copy-start
  0.0 1.9 %copy-done = f32[6,6,16384]{2,1,0:T(8,128)S(1)} copy-done((f32[6,6,16384]{2,1,0:T(8,128)S(1)}, f32[6,6,16384]{2,1,0:T(8,128)}, u32[]{:S(2)}) %copy-start) | copy-done | bytes 2359320
  1.9 52.7 %cov.1 = f32[6,48,1024]{2,1,0:T(8,128)S(1)} custom-call(f32[6,6,16384]{2,1,0:T(8,128)S(1)} %copy-done), custom_call_target="tpu_custom_call" | custom-call | tf_op jit(solution)/shard_map/cov/pallas_call | solution.py:183
  54.6 1.0 %copy.3 = f32[6,48,1024]{2,1,0:T(8,128)} copy(f32[6,48,1024]{2,1,0:T(8,128)S(1)} %cov.1) | data formatting | bytes 2359296
Async XLA Ops:
  0.0 1.9 %copy-start = (f32[6,6,16384]{2,1,0:T(8,128)S(1)}, f32[6,6,16384]{2,1,0:T(8,128)}, u32[]{:S(2)}) copy-start(f32[6,6,16384]{2,1,0:T(8,128)} %fields.1) | copy-start | bytes 7077892

commit v3 on v2

--- a/solution.py
+++ b/solution.py
@@ -9,20 +9,20 @@
 
 MESH = pl.DeviceIdType.MESH
 F32 = jnp.float32
-ORDER = ((1, 1), (3, 0), (1, 0), (3, 1), (0, 0), (2, 1), (0, 1), (2, 0))
+ORDER = ((2, 1), (0, 0), (2, 0), (0, 1), (1, 1), (3, 0), (1, 0), (3, 1))
 SELF = ORDER.index((0, 0))
 SENDS = (
-    (1, 1), (0, 9), (1, 0), (0, 8), (0, 3), (1, 10), (1, 13), (0, 5), (1, 4), (0, 12), (1, 3), (0, 10),
-    (1, 5), (0, 13), (1, 11), (0, 2), (0, 4), (1, 12), (1, 2), (0, 11), (0, 7), (1, 14), (0, 0), (1, 9),
-    (0, 14), (1, 7), (1, 6), (0, 15), (0, 6), (1, 15), (0, 1), (1, 8), (2, 0), (3, 9), (2, 1), (3, 8),
-    (2, 3), (3, 10), (3, 13), (2, 5), (3, 4), (2, 12), (3, 3), (2, 10), (3, 5), (2, 13), (3, 11), (2, 2),
-    (2, 4), (3, 12), (3, 2), (2, 11), (2, 7), (3, 14), (2, 14), (3, 7), (3, 1), (2, 9), (3, 6), (2, 15),
-    (2, 6), (3, 15), (3, 0), (2, 8), (5, 9), (4, 1), (5, 8), (4, 4), (5, 13), (4, 2), (5, 10), (4, 5),
-    (5, 12), (4, 13), (5, 5), (4, 3), (5, 11), (4, 12), (5, 4), (4, 15), (5, 7), (4, 6), (5, 14), (4, 7),
-    (5, 15), (4, 8), (5, 0), (4, 14), (5, 6), (4, 9), (5, 1), (5, 3), (4, 10), (4, 11), (5, 2), (6, 3),
-    (7, 10), (6, 2), (7, 11), (7, 7), (6, 14), (7, 0), (6, 9), (7, 14), (6, 7), (6, 1), (7, 9), (6, 6),
-    (7, 15), (7, 6), (6, 15), (6, 0), (7, 8), (7, 1), (6, 8), (7, 3), (6, 10), (6, 13), (7, 5), (6, 4),
-    (7, 12), (6, 5), (7, 13), (6, 11), (7, 2), (7, 4), (6, 12),
+    (0, 9), (1, 1), (0, 8), (1, 4), (0, 13), (1, 2), (0, 10), (1, 5), (0, 12), (1, 13), (0, 5), (1, 3),
+    (0, 11), (1, 12), (0, 4), (1, 15), (0, 7), (1, 6), (0, 14), (1, 7), (0, 15), (1, 8), (0, 0), (1, 14),
+    (0, 6), (1, 9), (0, 1), (0, 3), (1, 10), (1, 11), (0, 2), (3, 3), (2, 10), (3, 2), (2, 11), (2, 7),
+    (3, 14), (2, 0), (3, 9), (2, 14), (3, 7), (3, 1), (2, 9), (3, 6), (2, 15), (2, 6), (3, 15), (3, 0),
+    (2, 8), (2, 1), (3, 8), (2, 3), (3, 10), (3, 13), (2, 5), (3, 4), (2, 12), (3, 5), (2, 13), (3, 11),
+    (2, 2), (2, 4), (3, 12), (5, 1), (4, 9), (5, 0), (4, 8), (4, 3), (5, 10), (5, 13), (4, 5), (5, 4),
+    (4, 12), (5, 3), (4, 10), (5, 5), (4, 13), (5, 11), (4, 2), (4, 4), (5, 12), (5, 2), (4, 11), (4, 7),
+    (5, 14), (4, 0), (5, 9), (4, 14), (5, 7), (5, 6), (4, 15), (4, 6), (5, 15), (4, 1), (5, 8), (6, 0),
+    (7, 9), (6, 1), (7, 8), (6, 3), (7, 10), (7, 13), (6, 5), (7, 4), (6, 12), (7, 3), (6, 10), (7, 5),
+    (6, 13), (7, 11), (6, 2), (6, 4), (7, 12), (7, 2), (6, 11), (6, 7), (7, 14), (6, 14), (7, 7), (7, 1),
+    (6, 9), (7, 6), (6, 15), (6, 6), (7, 15), (7, 0), (6, 8),
 )
 
 
@@ -119,7 +119,7 @@
             src_ref=blk.at[a, b],
             dst_ref=got.at[m, from_m[b]],
             send_sem=send3,
-            recv_sem=recv3,
+            recv_sem=recv3.at[m],
             device_id=(t, from_m[a]),
             device_id_type=MESH,
         ).start()
@@ -152,23 +152,30 @@
                     pending.append((s2, s))
     for a, b in pending:
         ship(a, b)
+    def place(o, line):
+        lanes = pixels(o)
+
+        @pl.loop(0, rows)
+        def _(i):
+            for n in range(members):
+                out[i, n * rows:(n + 1) * rows, lanes] = line(n, i)
+
     for b in range(len(ORDER)):
         got[m, from_m[b]] = blk[SELF, b]
-
-    arrived = got.at[pl.ds(0, members - 1)]
-    done = pltpu.make_async_remote_copy(
-        src_ref=arrived, dst_ref=arrived, send_sem=send3, recv_sem=recv3,
+    for o in [m] + [from_m[b] for b in range(len(ORDER)) if b != SELF]:
+        if o is not m:
+            part = got.at[o]
+            pltpu.make_async_remote_copy(
+                src_ref=part, dst_ref=part, send_sem=send3, recv_sem=recv3.at[o],
+                device_id=(t, m), device_id_type=MESH,
+            ).wait_recv()
+        place(o, lambda n, i, o=o: got[o, n, i])
+
+    shipped = got.at[pl.ds(0, members - 1)]
+    pltpu.make_async_remote_copy(
+        src_ref=shipped, dst_ref=shipped, send_sem=send3, recv_sem=recv3.at[0],
         device_id=(t, m), device_id_type=MESH,
-    )
-    done.wait_recv()
-
-    @pl.loop(0, rows)
-    def _(i):
-        for o in range(members):
-            for n in range(members):
-                out[i, n * rows:(n + 1) * rows, o * 128:(o + 1) * 128] = got[o, n, i]
-
-    done.wait_send()
+    ).wait_send()
     sent = raw.at[pl.ds(0, total - 1)]
     pltpu.make_async_remote_copy(
         src_ref=sent, dst_ref=sent, send_sem=send1, recv_sem=recv1.at[0],
@@ -194,9 +201,9 @@
             pltpu.SemaphoreType.DMA((members,)),
             pltpu.SemaphoreType.DMA,
             pltpu.SemaphoreType.DMA,
-            pltpu.SemaphoreType.DMA,
+            pltpu.SemaphoreType.DMA((members,)),
         ],
-        compiler_params=pltpu.CompilerParams(collective_id=0, has_side_effects=True, vmem_limit_bytes=40 * 2**20),
+        compiler_params=pltpu.CompilerParams(collective_id=0, has_side_effects=True, vmem_limit_bytes=50 * 2**20),
         name="cov",
     )(fields)
 

time: 55.7 us -> 53.4 us (0.959)
  local copies, waits for them, and re-layouts: 2.9 us -> 1.02 us
    unnamed x3 -> x1, local copies, waits for them, and re-layouts: 2.9 us -> 1.02 us
where the time goes in v3:
time: 53.4 us; the launch traced here: 53.3 us
  Pallas kernels  52.3 us (98%)
  local copies, waits for them, and re-layouts  1.02 us (2%)
    pallas_call x1, Pallas kernels, per_device(): pl.pallas_call(functools.partial(kernel, (tms, members, rows, mons, scale...  52.3 us

profile of v3, /device:TPU:1, one launch (start us, length us, event | category | flops | bytes accessed | tf_op | source)
XLA Modules:
  0.0 53.3 jit_solution(7216385777545651202)
XLA Ops:
  0.0 52.3 %cov.1 = f32[6,48,1024]{2,1,0:T(8,128)S(1)} custom-call(f32[6,6,16384]{2,1,0:T(8,128)} %fields.1), custom_call_target="tpu_custom_call" | custom-call | tf_op jit(solution)/shard_map/cov/pallas_call | solution.py:190
  52.3 1.0 %copy.3 = f32[6,48,1024]{2,1,0:T(8,128)} copy(f32[6,48,1024]{2,1,0:T(8,128)S(1)} %cov.1) | data formatting | bytes 2359296

commit v4 on v3

--- a/solution.py
+++ b/solution.py
@@ -10,19 +10,20 @@
 MESH = pl.DeviceIdType.MESH
 F32 = jnp.float32
 ORDER = ((2, 1), (0, 0), (2, 0), (0, 1), (1, 1), (3, 0), (1, 0), (3, 1))
+EARLY = 7
 SELF = ORDER.index((0, 0))
 SENDS = (
-    (0, 9), (1, 1), (0, 8), (1, 4), (0, 13), (1, 2), (0, 10), (1, 5), (0, 12), (1, 13), (0, 5), (1, 3),
-    (0, 11), (1, 12), (0, 4), (1, 15), (0, 7), (1, 6), (0, 14), (1, 7), (0, 15), (1, 8), (0, 0), (1, 14),
-    (0, 6), (1, 9), (0, 1), (0, 3), (1, 10), (1, 11), (0, 2), (3, 3), (2, 10), (3, 2), (2, 11), (2, 7),
-    (3, 14), (2, 0), (3, 9), (2, 14), (3, 7), (3, 1), (2, 9), (3, 6), (2, 15), (2, 6), (3, 15), (3, 0),
-    (2, 8), (2, 1), (3, 8), (2, 3), (3, 10), (3, 13), (2, 5), (3, 4), (2, 12), (3, 5), (2, 13), (3, 11),
-    (2, 2), (2, 4), (3, 12), (5, 1), (4, 9), (5, 0), (4, 8), (4, 3), (5, 10), (5, 13), (4, 5), (5, 4),
-    (4, 12), (5, 3), (4, 10), (5, 5), (4, 13), (5, 11), (4, 2), (4, 4), (5, 12), (5, 2), (4, 11), (4, 7),
-    (5, 14), (4, 0), (5, 9), (4, 14), (5, 7), (5, 6), (4, 15), (4, 6), (5, 15), (4, 1), (5, 8), (6, 0),
-    (7, 9), (6, 1), (7, 8), (6, 3), (7, 10), (7, 13), (6, 5), (7, 4), (6, 12), (7, 3), (6, 10), (7, 5),
-    (6, 13), (7, 11), (6, 2), (6, 4), (7, 12), (7, 2), (6, 11), (6, 7), (7, 14), (6, 14), (7, 7), (7, 1),
-    (6, 9), (7, 6), (6, 15), (6, 6), (7, 15), (7, 0), (6, 8),
+    (0, 1), (1, 1), (0, 0), (2, 1), (3, 0), (2, 0), (3, 1), (1, 11), (0, 3), (1, 10), (0, 2), (0, 9),
+    (1, 5), (0, 15), (1, 6), (0, 14), (1, 14), (0, 5), (1, 8), (1, 3), (0, 11), (0, 8), (1, 13), (0, 4),
+    (1, 12), (1, 4), (0, 12), (0, 7), (1, 15), (0, 6), (1, 7), (0, 13), (1, 9), (1, 2), (0, 10), (3, 11),
+    (2, 3), (3, 10), (2, 2), (2, 9), (3, 5), (2, 15), (3, 6), (2, 14), (3, 14), (2, 5), (3, 8), (3, 3),
+    (2, 11), (2, 8), (3, 13), (2, 4), (3, 12), (3, 4), (2, 12), (2, 7), (3, 15), (2, 6), (3, 7), (2, 13),
+    (3, 9), (3, 2), (2, 10), (4, 3), (5, 10), (4, 7), (5, 14), (5, 13), (4, 5), (5, 4), (4, 12), (5, 3),
+    (4, 10), (4, 0), (5, 9), (4, 14), (5, 7), (5, 1), (4, 9), (5, 5), (4, 13), (5, 11), (4, 2), (5, 6),
+    (4, 15), (4, 4), (5, 12), (4, 6), (5, 15), (5, 2), (4, 11), (5, 0), (4, 8), (4, 1), (5, 8), (6, 3),
+    (7, 10), (6, 7), (7, 14), (7, 13), (6, 5), (7, 4), (6, 12), (7, 3), (6, 10), (6, 0), (7, 9), (6, 14),
+    (7, 7), (7, 1), (6, 9), (7, 5), (6, 13), (7, 11), (6, 2), (7, 6), (6, 15), (6, 4), (7, 12), (6, 6),
+    (7, 15), (7, 2), (6, 11), (7, 0), (6, 8), (6, 1), (7, 8),
 )
 
 
@@ -41,7 +42,7 @@
     return out
 
 
-def kernel(sizes, fields, out, raw, con, blk, got, send1, recv1, own, send3, recv3):
+def kernel(sizes, fields, out, raw, con, blk, got, send1, recv1, own, send3, recv3, ready):
     tms, members, rows, mons, scale = sizes
     t, m = lax.axis_index("tm"), lax.axis_index("member")
     me = t * members + m
@@ -55,8 +56,24 @@
     from_m = [((x + dx) % 4) * 2 + (h + dh) % 2 for dx, dh in ORDER]
     to_m = [((x + 4 - dx) % 4) * 2 + (h + dh) % 2 for dx, dh in ORDER]
 
-    for s, q in SENDS:
-        pl.semaphore_signal(barrier, inc=1, device_id=(near_t[q], to_m[s]), device_id_type=MESH)
+    def greet(other_t, other_m):
+        pl.semaphore_signal(barrier, inc=1, device_id=(other_t, other_m), device_id_type=MESH)
+
+    twin = t + 1 - 2 * core
+    for s in range(len(ORDER)):
+        for q in range(0, 4, 2):
+            seen = near_t[q] - core
+            if s == SELF and q == 0:
+                pl.when(core == 1)(functools.partial(greet, seen, m))
+            else:
+                greet(seen, to_m[s])
+    for s in range(len(ORDER)):
+        for q in range(0, tms, 2):
+            seen = near_t[q] + 1 - core
+            if s == SELF and q == 0:
+                pl.when(core == 0)(functools.partial(greet, seen, m))
+            else:
+                greet(seen, to_m[s])
 
     def pixels(d):
         return pl.ds(pl.multiple_of(d * 128, 128), 128)
@@ -64,13 +81,7 @@
     mine = pltpu.make_async_copy(fields.at[:, :, pixels(me)], raw.at[SELF * tms + t], own)
     mine.start()
 
-    @pl.loop(0, con.shape[0])
-    def _(s):
-        con[s] = jnp.zeros(con.shape[1:], F32)
-
-    pl.semaphore_wait(barrier, total - 1)
-
-    for s, q in SENDS:
+    def send(s, q):
         pltpu.make_async_remote_copy(
             src_ref=fields.at[:, :, pixels(near_t[q] * members + to_m[s])],
             dst_ref=raw.at[s * tms + t],
@@ -79,6 +90,34 @@
             device_id=(near_t[q], to_m[s]),
             device_id_type=MESH,
         ).start()
+
+    @pl.when(core == 0)
+    def _():
+        pl.semaphore_wait(barrier, 4 * members - 1)
+        pl.semaphore_signal(ready, inc=1, device_id=(twin, m), device_id_type=MESH)
+
+    @pl.when(core == 1)
+    def _():
+        pl.semaphore_wait(ready, 1)
+
+    for s, q in SENDS[:EARLY]:
+        send(s, q)
+
+    @pl.when(core == 1)
+    def _():
+        pl.semaphore_wait(barrier, total - 1)
+        pl.semaphore_signal(ready, inc=1, device_id=(twin, m), device_id_type=MESH)
+
+    @pl.when(core == 0)
+    def _():
+        pl.semaphore_wait(ready, 1)
+
+    for s, q in SENDS[EARLY:]:
+        send(s, q)
+
+    @pl.loop(0, con.shape[0])
+    def _(s):
+        con[s] = jnp.zeros(con.shape[1:], F32)
 
     def transform(s):
         @pl.loop(0, rows)
@@ -202,6 +241,7 @@
             pltpu.SemaphoreType.DMA,
             pltpu.SemaphoreType.DMA,
             pltpu.SemaphoreType.DMA((members,)),
+            pltpu.SemaphoreType.REGULAR,
         ],
         compiler_params=pltpu.CompilerParams(collective_id=0, has_side_effects=True, vmem_limit_bytes=50 * 2**20),
         name="cov",

time: 53.4 us -> 51.6 us (0.966)
  Pallas kernels: 52.3 us -> 50.2 us
    pallas_call x1, Pallas kernels: 52.3 us -> 50.2 us  [per_device(): pl.pallas_call(functools.partial(kernel, (tms, members, rows, mons, scale...]
where the time goes in v4:
time: 51.6 us; the launch traced here: 51.2 us
  Pallas kernels  50.2 us (97%)
  local copies, waits for them, and re-layouts  1.02 us (2%)
    pallas_call x1, Pallas kernels, per_device(): pl.pallas_call(functools.partial(kernel, (tms, members, rows, mons, scale...  50.2 us

profile of v4, /device:TPU:1, one launch (start us, length us, event | category | flops | bytes accessed | tf_op | source)
XLA Modules:
  0.0 51.2 jit_solution(5078746207156410252)
XLA Ops:
  0.0 50.2 %cov.1 = f32[6,48,1024]{2,1,0:T(8,128)S(1)} custom-call(f32[6,6,16384]{2,1,0:T(8,128)} %fields.1), custom_call_target="tpu_custom_call" | custom-call | tf_op jit(solution)/shard_map/cov/pallas_call | solution.py:229
  50.2 1.0 %copy.3 = f32[6,48,1024]{2,1,0:T(8,128)} copy(f32[6,48,1024]{2,1,0:T(8,128)S(1)} %cov.1) | data formatting | bytes 2359296

commit v5 on v4

--- a/solution.py
+++ b/solution.py
@@ -10,20 +10,20 @@
 MESH = pl.DeviceIdType.MESH
 F32 = jnp.float32
 ORDER = ((2, 1), (0, 0), (2, 0), (0, 1), (1, 1), (3, 0), (1, 0), (3, 1))
-EARLY = 7
+EARLY = 8
 SELF = ORDER.index((0, 0))
 SENDS = (
-    (0, 1), (1, 1), (0, 0), (2, 1), (3, 0), (2, 0), (3, 1), (1, 11), (0, 3), (1, 10), (0, 2), (0, 9),
-    (1, 5), (0, 15), (1, 6), (0, 14), (1, 14), (0, 5), (1, 8), (1, 3), (0, 11), (0, 8), (1, 13), (0, 4),
-    (1, 12), (1, 4), (0, 12), (0, 7), (1, 15), (0, 6), (1, 7), (0, 13), (1, 9), (1, 2), (0, 10), (3, 11),
-    (2, 3), (3, 10), (2, 2), (2, 9), (3, 5), (2, 15), (3, 6), (2, 14), (3, 14), (2, 5), (3, 8), (3, 3),
-    (2, 11), (2, 8), (3, 13), (2, 4), (3, 12), (3, 4), (2, 12), (2, 7), (3, 15), (2, 6), (3, 7), (2, 13),
-    (3, 9), (3, 2), (2, 10), (4, 3), (5, 10), (4, 7), (5, 14), (5, 13), (4, 5), (5, 4), (4, 12), (5, 3),
-    (4, 10), (4, 0), (5, 9), (4, 14), (5, 7), (5, 1), (4, 9), (5, 5), (4, 13), (5, 11), (4, 2), (5, 6),
-    (4, 15), (4, 4), (5, 12), (4, 6), (5, 15), (5, 2), (4, 11), (5, 0), (4, 8), (4, 1), (5, 8), (6, 3),
-    (7, 10), (6, 7), (7, 14), (7, 13), (6, 5), (7, 4), (6, 12), (7, 3), (6, 10), (6, 0), (7, 9), (6, 14),
-    (7, 7), (7, 1), (6, 9), (7, 5), (6, 13), (7, 11), (6, 2), (7, 6), (6, 15), (6, 4), (7, 12), (6, 6),
-    (7, 15), (7, 2), (6, 11), (7, 0), (6, 8), (6, 1), (7, 8),
+    (4, 3), (5, 3), (1, 3), (0, 3), (2, 3), (3, 3), (7, 3), (6, 3), (0, 8), (1, 1), (0, 9), (1, 4),
+    (0, 12), (1, 12), (0, 4), (1, 13), (0, 5), (1, 9), (0, 0), (1, 8), (0, 1), (1, 5), (0, 13), (1, 10),
+    (0, 2), (1, 11), (0, 6), (1, 15), (0, 11), (1, 2), (0, 10), (1, 6), (0, 15), (1, 7), (0, 14), (1, 14),
+    (0, 7), (3, 9), (2, 0), (3, 11), (2, 2), (2, 8), (3, 1), (2, 11), (3, 2), (2, 9), (3, 0), (3, 10),
+    (2, 7), (3, 15), (2, 6), (3, 13), (2, 13), (3, 4), (2, 4), (3, 14), (2, 10), (2, 1), (3, 8), (3, 6),
+    (2, 14), (3, 5), (2, 12), (3, 12), (2, 5), (3, 7), (2, 15), (5, 9), (4, 0), (5, 11), (4, 2), (4, 8),
+    (5, 1), (4, 11), (5, 2), (4, 9), (5, 0), (5, 10), (4, 7), (5, 15), (4, 6), (5, 13), (4, 13), (5, 4),
+    (4, 4), (5, 14), (4, 10), (4, 1), (5, 8), (5, 6), (4, 14), (5, 5), (4, 12), (5, 12), (4, 5), (5, 7),
+    (4, 15), (7, 9), (6, 0), (7, 11), (6, 2), (6, 8), (7, 1), (6, 11), (7, 2), (6, 9), (7, 0), (7, 10),
+    (6, 7), (7, 15), (6, 6), (7, 13), (6, 13), (7, 4), (6, 4), (7, 14), (6, 10), (6, 1), (7, 8), (7, 6),
+    (6, 14), (7, 5), (6, 12), (7, 12), (6, 5), (7, 7), (6, 15),
 )
 
 
@@ -151,12 +151,23 @@
         for b in range(rows):
             blk[s2, s, b] = cols[b][0:rows]
 
+    def pack(s):
+        r3, r4, r5 = (blk[s, s, i] for i in range(3, 6))
+        blk[s, s, 3] = jnp.concatenate([r3[3:6], r4[4:6], r5[5:6]], axis=0)
+
+    def unpack(o):
+        top = [got[o, m * rows + i] for i in range(3)]
+        low = got[o, m * rows + 3]
+        for i, rest in ((3, [low[0:3]]), (4, [low[1:2], low[3:5]]), (5, [low[2:3], low[4:6]])):
+            got[o, m * rows + i] = jnp.concatenate([r[i:i + 1] for r in top] + rest, axis=0)
+
     def ship(a, b):
         if a == SELF:
             return
+        lines = 4 if a == b else rows
         pltpu.make_async_remote_copy(
-            src_ref=blk.at[a, b],
-            dst_ref=got.at[m, from_m[b]],
+            src_ref=blk.at[a, b, pl.ds(0, lines)],
+            dst_ref=got.at[m, pl.ds(from_m[b] * rows, lines)],
             send_sem=send3,
             recv_sem=recv3.at[m],
             device_id=(t, from_m[a]),
@@ -182,6 +193,8 @@
             def _(s2, s=s):
                 block(s, s2)
 
+            if hi == s + 1 and s != SELF:
+                pack(s)
             for a, b in pending:
                 ship(a, b)
             pending = []
@@ -200,17 +213,18 @@
                 out[i, n * rows:(n + 1) * rows, lanes] = line(n, i)
 
     for b in range(len(ORDER)):
-        got[m, from_m[b]] = blk[SELF, b]
+        got[m, pl.ds(from_m[b] * rows, rows)] = blk[SELF, b]
     for o in [m] + [from_m[b] for b in range(len(ORDER)) if b != SELF]:
         if o is not m:
-            part = got.at[o]
+            part = got.at[o, pl.ds(0, members * rows - 2)]
             pltpu.make_async_remote_copy(
                 src_ref=part, dst_ref=part, send_sem=send3, recv_sem=recv3.at[o],
                 device_id=(t, m), device_id_type=MESH,
             ).wait_recv()
-        place(o, lambda n, i, o=o: got[o, n, i])
-
-    shipped = got.at[pl.ds(0, members - 1)]
+            unpack(o)
+        place(o, lambda n, i, o=o: got[o, n * rows + i])
+
+    shipped = got.at[pl.ds(0, members - 1), pl.ds(0, members * rows - 2)]
     pltpu.make_async_remote_copy(
         src_ref=shipped, dst_ref=shipped, send_sem=send3, recv_sem=recv3.at[0],
         device_id=(t, m), device_id_type=MESH,
@@ -235,7 +249,7 @@
             pltpu.VMEM((tms * members, rows, mons, 128), F32),
             pltpu.VMEM((members, 14, rows, 8, 128), F32),
             pltpu.VMEM((members, members, rows, rows, 128), F32),
-            pltpu.VMEM((members, members, rows, rows, 128), F32),
+            pltpu.VMEM((members, members * rows, rows, 128), F32),
             pltpu.SemaphoreType.DMA,
             pltpu.SemaphoreType.DMA((members,)),
             pltpu.SemaphoreType.DMA,

time: 51.6 us -> 50.8 us (0.984)
  no operation moved by 1% of the time
where the time goes in v5:
time: 50.8 us; the launch traced here: 50.7 us
  Pallas kernels  49.7 us (98%)
  local copies, waits for them, and re-layouts  1.02 us (2%)
    pallas_call x1, Pallas kernels, per_device(): pl.pallas_call(functools.partial(kernel, (tms, members, rows, mons, scale...  49.7 us

profile of v5, /device:TPU:1, one launch (start us, length us, event | category | flops | bytes accessed | tf_op | source)
XLA Modules:
  0.0 50.7 jit_solution(1464328419577730415)
XLA Ops:
  0.0 49.7 %cov.1 = f32[6,48,1024]{2,1,0:T(8,128)S(1)} custom-call(f32[6,6,16384]{2,1,0:T(8,128)} %fields.1), custom_call_target="tpu_custom_call" | custom-call | tf_op jit(solution)/shard_map/cov/pallas_call | solution.py:243
  49.7 1.0 %copy.3 = f32[6,48,1024]{2,1,0:T(8,128)} copy(f32[6,48,1024]{2,1,0:T(8,128)S(1)} %cov.1) | data formatting | bytes 2359296

commit v6 on v5

--- a/solution.py
+++ b/solution.py
@@ -10,12 +10,11 @@
 MESH = pl.DeviceIdType.MESH
 F32 = jnp.float32
 ORDER = ((2, 1), (0, 0), (2, 0), (0, 1), (1, 1), (3, 0), (1, 0), (3, 1))
-EARLY = 8
 SELF = ORDER.index((0, 0))
 SENDS = (
-    (4, 3), (5, 3), (1, 3), (0, 3), (2, 3), (3, 3), (7, 3), (6, 3), (0, 8), (1, 1), (0, 9), (1, 4),
-    (0, 12), (1, 12), (0, 4), (1, 13), (0, 5), (1, 9), (0, 0), (1, 8), (0, 1), (1, 5), (0, 13), (1, 10),
-    (0, 2), (1, 11), (0, 6), (1, 15), (0, 11), (1, 2), (0, 10), (1, 6), (0, 15), (1, 7), (0, 14), (1, 14),
+    (4, 3), (5, 3), (1, 3), (0, 3), (2, 3), (3, 3), (7, 3), (6, 3), (0, 8), (1, 1), (0, 9), (1, 12),
+    (0, 4), (1, 4), (0, 12), (1, 13), (0, 5), (1, 8), (0, 1), (1, 9), (0, 0), (1, 5), (0, 13), (1, 10),
+    (0, 2), (1, 11), (0, 6), (1, 15), (0, 10), (1, 2), (0, 11), (1, 6), (0, 14), (1, 7), (0, 15), (1, 14),
     (0, 7), (3, 9), (2, 0), (3, 11), (2, 2), (2, 8), (3, 1), (2, 11), (3, 2), (2, 9), (3, 0), (3, 10),
     (2, 7), (3, 15), (2, 6), (3, 13), (2, 13), (3, 4), (2, 4), (3, 14), (2, 10), (2, 1), (3, 8), (3, 6),
     (2, 14), (3, 5), (2, 12), (3, 12), (2, 5), (3, 7), (2, 15), (5, 9), (4, 0), (5, 11), (4, 2), (4, 8),
@@ -24,6 +23,13 @@
     (4, 15), (7, 9), (6, 0), (7, 11), (6, 2), (6, 8), (7, 1), (6, 11), (7, 2), (6, 9), (7, 0), (7, 10),
     (6, 7), (7, 15), (6, 6), (7, 13), (6, 13), (7, 4), (6, 4), (7, 14), (6, 10), (6, 1), (7, 8), (7, 6),
     (6, 14), (7, 5), (6, 12), (7, 12), (6, 5), (7, 7), (6, 15),
+)
+FIRST = (
+    4, 4, 4, 4, 4, 4, 4, 4, 0, 0, 0, 0, 0, 0, 0, 0, 0, 0, 0, 0, 1, 0, 0, 0, 0, 0, 0, 0, 0, 0,
+    0, 0, 0, 0, 0, 0, 0, 0, 1, 0, 0, 0, 0, 0, 0, 0, 2, 0, 0, 0, 0, 0, 0, 0, 0, 0, 0, 0, 0, 0,
+    0, 0, 0, 0, 0, 0, 0, 0, 0, 0, 0, 0, 0, 0, 0, 0, 0, 0, 0, 0, 0, 0, 0, 0, 0, 0, 0, 0, 0, 0,
+    0, 0, 0, 0, 0, 0, 0, 0, 0, 0, 0, 0, 0, 0, 0, 0, 0, 0, 0, 0, 0, 0, 0, 0, 0, 0, 0, 0, 0, 0,
+    0, 0, 0, 0, 0, 0, 0,
 )
 
 
@@ -100,8 +106,9 @@
     def _():
         pl.semaphore_wait(ready, 1)
 
-    for s, q in SENDS[:EARLY]:
-        send(s, q)
+    for (s, q), first in zip(SENDS, FIRST):
+        if first > 0:
+            pl.when(ten < first)(functools.partial(send, s, q))
 
     @pl.when(core == 1)
     def _():
@@ -112,20 +119,26 @@
     def _():
         pl.semaphore_wait(ready, 1)
 
-    for s, q in SENDS[EARLY:]:
-        send(s, q)
+    for (s, q), first in zip(SENDS, FIRST):
+        if first < 4:
+            pl.when(ten >= first)(functools.partial(send, s, q))
 
     @pl.loop(0, con.shape[0])
     def _(s):
-        con[s] = jnp.zeros(con.shape[1:], F32)
+        con[s, 9:11] = jnp.zeros((2, *con.shape[2:]), F32)
 
     def transform(s):
         @pl.loop(0, rows)
         def _(i):
+            cs = []
             for half in range(2):
-                years = [raw[s * tms + 2 * y + half, i] for y in range(tms // 2)]
-                for q, c in enumerate(contrasts(years)):
-                    con[s, half * 7 + q, i, 0:mons] = c
+                cs += contrasts([raw[s * tms + 2 * y + half, i] for y in range(tms // 2)])
+            for g in range(3):
+                for k in range(3):
+                    con[s, 3 * g + k, i, 0:mons] = cs[4 * g + k]
+                    con[s, 3 * g + k, i, mons:8] = cs[4 * g + 3][2 * k:2 * k + 2]
+            for k in range(2):
+                con[s, 9 + k, i, 0:mons] = cs[12 + k]
 
     lane_row = lax.broadcasted_iota(jnp.int32, (8, 128), 0)
 
@@ -133,7 +146,7 @@
         cols = [jnp.zeros((8, 128), F32) for _ in range(rows)]
         for base in range(0, rows, 3):
             acc = [[None] * rows for _ in range(3)]
-            for q in range(14):
+            for q in range(11):
                 left = [con[s, q, base + a] for a in range(3)]
                 right = [con[s2, q, b] for b in range(rows)]
                 for a in range(3):
@@ -247,7 +260,7 @@
         out_specs=pl.BlockSpec(memory_space=pltpu.VMEM),
         scratch_shapes=[
             pltpu.VMEM((tms * members, rows, mons, 128), F32),
-            pltpu.VMEM((members, 14, rows, 8, 128), F32),
+            pltpu.VMEM((members, 11, rows, 8, 128), F32),
             pltpu.VMEM((members, members, rows, rows, 128), F32),
             pltpu.VMEM((members, members * rows, rows, 128), F32),
             pltpu.SemaphoreType.DMA,

time: 50.8 us -> 50.2 us (0.988)
  Pallas kernels: 49.7 us -> 49.1 us
    pallas_call x1, Pallas kernels: 49.7 us -> 49.1 us  [per_device(): pl.pallas_call(functools.partial(kernel, (tms, members, rows, mons, scale...]
where the time goes in v6:
time: 50.2 us; the launch traced here: 50.1 us
  Pallas kernels  49.1 us (98%)
  local copies, waits for them, and re-layouts  1.02 us (2%)
    pallas_call x1, Pallas kernels, per_device(): pl.pallas_call(functools.partial(kernel, (tms, members, rows, mons, scale...  49.1 us
    unnamed x1, local copies, waits for them, and re-layouts  1.02 us

profile of v6, /device:TPU:1, one launch (start us, length us, event | category | flops | bytes accessed | tf_op | source)
XLA Modules:
  0.0 50.1 jit_solution(13788650944131406117)
XLA Ops:
  0.0 49.1 %cov.1 = f32[6,48,1024]{2,1,0:T(8,128)S(1)} custom-call(f32[6,6,16384]{2,1,0:T(8,128)} %fields.1), custom_call_target="tpu_custom_call" | custom-call | tf_op jit(solution)/shard_map/cov/pallas_call | solution.py:256
  49.1 1.0 %copy.3 = f32[6,48,1024]{2,1,0:T(8,128)} copy(f32[6,48,1024]{2,1,0:T(8,128)S(1)} %cov.1) | data formatting | bytes 2359296

commit v7 on v6

--- a/solution.py
+++ b/solution.py
@@ -9,12 +9,12 @@
 
 MESH = pl.DeviceIdType.MESH
 F32 = jnp.float32
-ORDER = ((2, 1), (0, 0), (2, 0), (0, 1), (1, 1), (3, 0), (1, 0), (3, 1))
+ORDER = ((2, 1), (0, 0), (2, 0), (0, 1), (1, 0), (3, 1), (3, 0), (1, 1))
 SELF = ORDER.index((0, 0))
 SENDS = (
-    (4, 3), (5, 3), (1, 3), (0, 3), (2, 3), (3, 3), (7, 3), (6, 3), (0, 8), (1, 1), (0, 9), (1, 12),
-    (0, 4), (1, 4), (0, 12), (1, 13), (0, 5), (1, 8), (0, 1), (1, 9), (0, 0), (1, 5), (0, 13), (1, 10),
-    (0, 2), (1, 11), (0, 6), (1, 15), (0, 10), (1, 2), (0, 11), (1, 6), (0, 14), (1, 7), (0, 15), (1, 14),
+    (7, 3), (6, 3), (1, 3), (0, 3), (2, 3), (3, 3), (5, 3), (4, 3), (0, 8), (1, 1), (0, 9), (1, 4),
+    (0, 12), (1, 12), (0, 4), (1, 13), (0, 5), (1, 9), (0, 0), (1, 8), (0, 1), (1, 5), (0, 13), (1, 10),
+    (0, 2), (1, 11), (0, 6), (1, 15), (0, 11), (1, 2), (0, 10), (1, 6), (0, 15), (1, 7), (0, 14), (1, 14),
     (0, 7), (3, 9), (2, 0), (3, 11), (2, 2), (2, 8), (3, 1), (2, 11), (3, 2), (2, 9), (3, 0), (3, 10),
     (2, 7), (3, 15), (2, 6), (3, 13), (2, 13), (3, 4), (2, 4), (3, 14), (2, 10), (2, 1), (3, 8), (3, 6),
     (2, 14), (3, 5), (2, 12), (3, 12), (2, 5), (3, 7), (2, 15), (5, 9), (4, 0), (5, 11), (4, 2), (4, 8),
@@ -25,8 +25,8 @@
     (6, 14), (7, 5), (6, 12), (7, 12), (6, 5), (7, 7), (6, 15),
 )
 FIRST = (
-    4, 4, 4, 4, 4, 4, 4, 4, 0, 0, 0, 0, 0, 0, 0, 0, 0, 0, 0, 0, 1, 0, 0, 0, 0, 0, 0, 0, 0, 0,
-    0, 0, 0, 0, 0, 0, 0, 0, 1, 0, 0, 0, 0, 0, 0, 0, 2, 0, 0, 0, 0, 0, 0, 0, 0, 0, 0, 0, 0, 0,
+    4, 4, 4, 4, 4, 4, 4, 4, 0, 0, 0, 0, 0, 0, 0, 0, 0, 0, 1, 0, 0, 0, 0, 0, 0, 0, 0, 0, 0, 0,
+    0, 0, 0, 0, 0, 0, 0, 0, 1, 0, 0, 0, 0, 0, 0, 0, 0, 0, 0, 0, 0, 0, 0, 0, 0, 0, 0, 0, 0, 0,
     0, 0, 0, 0, 0, 0, 0, 0, 0, 0, 0, 0, 0, 0, 0, 0, 0, 0, 0, 0, 0, 0, 0, 0, 0, 0, 0, 0, 0, 0,
     0, 0, 0, 0, 0, 0, 0, 0, 0, 0, 0, 0, 0, 0, 0, 0, 0, 0, 0, 0, 0, 0, 0, 0, 0, 0, 0, 0, 0, 0,
     0, 0, 0, 0, 0, 0, 0,
@@ -198,7 +198,7 @@
             device_id=(t, m), device_id_type=MESH,
         ).wait_recv()
         transform(s)
-        step = 4
+        step = 3
         for lo in range(0, s + 1, step):
             hi = min(lo + step, s + 1)
 

time: 50.2 us -> 49.8 us (level)
  no operation moved by 1% of the time
where the time goes in v7:
time: 49.8 us; the launch traced here: 49.7 us
  Pallas kernels  48.7 us (98%)
  local copies, waits for them, and re-layouts  1.02 us (2%)
    pallas_call x1, Pallas kernels, per_device(): pl.pallas_call(functools.partial(kernel, (tms, members, rows, mons, scale...  48.7 us
    unnamed x1, local copies, waits for them, and re-layouts  1.02 us

profile of v7, /device:TPU:1, one launch (start us, length us, event | category | flops | bytes accessed | tf_op | source)
XLA Modules:
  0.0 49.7 jit_solution(14394973252802437452)
XLA Ops:
  0.0 48.7 %cov.1 = f32[6,48,1024]{2,1,0:T(8,128)S(1)} custom-call(f32[6,6,16384]{2,1,0:T(8,128)} %fields.1), custom_call_target="tpu_custom_call" | custom-call | tf_op jit(solution)/shard_map/cov/pallas_call | solution.py:256
  48.7 1.0 %copy.3 = f32[6,48,1024]{2,1,0:T(8,128)} copy(f32[6,48,1024]{2,1,0:T(8,128)S(1)} %cov.1) | data formatting | bytes 2359296

commit v8 on v7

--- a/solution.py
+++ b/solution.py
@@ -25,8 +25,8 @@
     (6, 14), (7, 5), (6, 12), (7, 12), (6, 5), (7, 7), (6, 15),
 )
 FIRST = (
-    4, 4, 4, 4, 4, 4, 4, 4, 0, 0, 0, 0, 0, 0, 0, 0, 0, 0, 1, 0, 0, 0, 0, 0, 0, 0, 0, 0, 0, 0,
-    0, 0, 0, 0, 0, 0, 0, 0, 1, 0, 0, 0, 0, 0, 0, 0, 0, 0, 0, 0, 0, 0, 0, 0, 0, 0, 0, 0, 0, 0,
+    4, 4, 4, 4, 4, 4, 4, 4, 0, 0, 0, 0, 0, 0, 0, 0, 0, 0, 0, 0, 1, 0, 0, 0, 0, 0, 0, 0, 0, 0,
+    0, 0, 0, 0, 0, 0, 0, 0, 0, 0, 0, 0, 0, 0, 0, 0, 0, 0, 0, 0, 0, 0, 0, 0, 0, 0, 0, 1, 0, 0,
     0, 0, 0, 0, 0, 0, 0, 0, 0, 0, 0, 0, 0, 0, 0, 0, 0, 0, 0, 0, 0, 0, 0, 0, 0, 0, 0, 0, 0, 0,
     0, 0, 0, 0, 0, 0, 0, 0, 0, 0, 0, 0, 0, 0, 0, 0, 0, 0, 0, 0, 0, 0, 0, 0, 0, 0, 0, 0, 0, 0,
     0, 0, 0, 0, 0, 0, 0,

time: 49.8 us -> 49.8 us (level)
  no operation moved by 1% of the time
where the time goes in v8:
time: 49.8 us; the launch traced here: 49.7 us
  Pallas kernels  48.7 us (98%)
  local copies, waits for them, and re-layouts  1.02 us (2%)
    pallas_call x1, Pallas kernels, per_device(): pl.pallas_call(functools.partial(kernel, (tms, members, rows, mons, scale...  48.7 us
    unnamed x1, local copies, waits for them, and re-layouts  1.02 us

profile of v8, /device:TPU:1, one launch (start us, length us, event | category | flops | bytes accessed | tf_op | source)
XLA Modules:
  0.0 49.7 jit_solution(9168565655947738377)
XLA Ops:
  0.0 48.7 %cov.1 = f32[6,48,1024]{2,1,0:T(8,128)S(1)} custom-call(f32[6,6,16384]{2,1,0:T(8,128)} %fields.1), custom_call_target="tpu_custom_call" | custom-call | tf_op jit(solution)/shard_map/cov/pallas_call | solution.py:256
  48.7 1.0 %copy.3 = f32[6,48,1024]{2,1,0:T(8,128)} copy(f32[6,48,1024]{2,1,0:T(8,128)S(1)} %cov.1) | data formatting | bytes 2359296

commit v9 on v8

--- a/solution.py
+++ b/solution.py
@@ -26,7 +26,7 @@
 )
 FIRST = (
     4, 4, 4, 4, 4, 4, 4, 4, 0, 0, 0, 0, 0, 0, 0, 0, 0, 0, 0, 0, 1, 0, 0, 0, 0, 0, 0, 0, 0, 0,
-    0, 0, 0, 0, 0, 0, 0, 0, 0, 0, 0, 0, 0, 0, 0, 0, 0, 0, 0, 0, 0, 0, 0, 0, 0, 0, 0, 1, 0, 0,
+    0, 0, 0, 0, 0, 0, 0, 0, 0, 0, 0, 0, 0, 0, 1, 0, 0, 0, 0, 0, 0, 0, 0, 0, 0, 0, 0, 1, 0, 0,
     0, 0, 0, 0, 0, 0, 0, 0, 0, 0, 0, 0, 0, 0, 0, 0, 0, 0, 0, 0, 0, 0, 0, 0, 0, 0, 0, 0, 0, 0,
     0, 0, 0, 0, 0, 0, 0, 0, 0, 0, 0, 0, 0, 0, 0, 0, 0, 0, 0, 0, 0, 0, 0, 0, 0, 0, 0, 0, 0, 0,
     0, 0, 0, 0, 0, 0, 0,

time: 49.8 us -> 49.8 us (level)
  no operation moved by 1% of the time
where the time goes in v9:
time: 49.8 us; the launch traced here: 49.7 us
  Pallas kernels  48.7 us (98%)
  local copies, waits for them, and re-layouts  1.02 us (2%)
    pallas_call x1, Pallas kernels, per_device(): pl.pallas_call(functools.partial(kernel, (tms, members, rows, mons, scale...  48.7 us
    unnamed x1, local copies, waits for them, and re-layouts  1.02 us

profile of v9, /device:TPU:1, one launch (start us, length us, event | category | flops | bytes accessed | tf_op | source)
XLA Modules:
  0.0 49.7 jit_solution(17284298807057278877)
XLA Ops:
  0.0 48.7 %cov.1 = f32[6,48,1024]{2,1,0:T(8,128)S(1)} custom-call(f32[6,6,16384]{2,1,0:T(8,128)} %fields.1), custom_call_target="tpu_custom_call" | custom-call | tf_op jit(solution)/shard_map/cov/pallas_call | solution.py:256
  48.7 1.0 %copy.3 = f32[6,48,1024]{2,1,0:T(8,128)} copy(f32[6,48,1024]{2,1,0:T(8,128)S(1)} %cov.1) | data formatting | bytes 2359296
